TPU v7x, 32 devices: a whole 2x2x4 slice. The times are simulated.
32 devices in a mesh: band: 4 (over z), px: 4 (over x, core), py: 2 (over y).
Axes of the slice: x: 2, y: 2, z: 4, core: 2. Of those that a mesh axis runs over, the one named last changes fastest.
Arguments:
- orbitals: bfloat16 [4, 1024, 384], P('band', ('px', 'py')), may hold values from -0.01171875 to 0.01171875
- occupations: float32 [4], P('band'), may hold values from 0.2 to 2
- stick_map: int32 [2, 1024], P(None, 'px'), may hold values from 0 to 191, as said below
- core_density: float32 [192, 192, 192], P('py', 'px'), may hold values from 0.05 to 0.5
Outputs:
- potential: float32 [192, 192, 192], P('py', 'px')
- gradient: float32 [3, 192, 192, 192], P(None, 'py', 'px')
Inputs may be any that keep to these rules, and one draw needn't show every extreme that they name: `stick_map`: columns i * 128 * 2 to (i + 1) * 128 * 2 - 1 have x index from i * 48 to (i + 1) * 48 - 1; no two columns share a grid position.
All inputs are finite; a program needn't handle non-finite values.
Results may differ from a plain program's by a relative error of at most 0.0054.
Values may be sent and summed in bfloat16 or wider, within the bound.
No kernel may reach another device: no remote copies, remote signals or barrier semaphores. Data moves between devices by JAX's collectives and lax.ppermute only.
A program may use at most 128 MiB of HBM per device.

v0:
```python
import math
import jax
import jax.numpy as jnp
from jax import lax
from jax.sharding import PartitionSpec as P

SPACING = 0.25
PBE_KAPPA = 0.804
PBE_MU = 0.2195
SLATER_COEF = 0.75 * (3.0 / math.pi) ** (1.0 / 3.0)
REDUCED_SCALE = 4.0 * (3.0 * math.pi**2) ** (2.0 / 3.0)
HIGHEST_PREC = lax.Precision.HIGHEST


def complex_table(row_index, col_index, points, direction):
    product = row_index[:, None] * col_index[None, :] % points
    angles = 2.0 * math.pi / points * product.astype(jnp.float32)
    cosine = jnp.cos(angles)
    sine_part = direction * jnp.sin(angles)
    return jnp.stack([jnp.stack([cosine, sine_part], 1), jnp.stack([-sine_part, cosine], 1)], 0)


def freq_pair(positions, points):
    signed = jnp.where(positions <= points // 2, positions, positions - points).astype(jnp.float32)
    gradient_freq = jnp.where(positions == points // 2, 0.0, signed)
    return (signed, gradient_freq)


def swap_rows(values):
    return lax.all_to_all(values, "px", split_axis=1, concat_axis=0, tiled=True)


def swap_depth(values):
    moved = lax.all_to_all(values, ("band", "py"), split_axis=1, concat_axis=0, tiled=True)
    return moved


def exchange_part(density, fields):
    cube_root = jnp.cbrt(density)
    four_thirds = density * cube_root
    grad_square = fields[1] * fields[1] + fields[2] * fields[2] + fields[3] * fields[3]
    reduced = grad_square / (REDUCED_SCALE * four_thirds * four_thirds)
    denominator = 1.0 + PBE_MU * reduced / PBE_KAPPA
    enhance = 1.0 + PBE_KAPPA - PBE_KAPPA / denominator
    enhance_slope = PBE_MU / (denominator * denominator)
    potential = fields[0] - SLATER_COEF * cube_root * (
        4.0 / 3.0 * enhance - 8.0 / 3.0 * reduced * enhance_slope
    )
    return jnp.concatenate([potential[None], fields[1:]], 0)


def transform(rho_local, pieces, depth_index, px_index):
    zshare, y_rows, points = rho_local.shape
    rows_px = lax.axis_size("px")
    rows_py = lax.axis_size("py")
    xblock = points // rows_px
    kyblock = points // pieces
    zblock = zshare * (pieces // rows_py)
    every_index = jnp.arange(points, dtype=jnp.int32)
    forward = complex_table(every_index, every_index, points, -1.0)
    x_table = forward[0].reshape(points, 2, rows_px, xblock).transpose(0, 2, 1, 3)
    section_data = jnp.einsum("zyx,xbsk->ybzsk", rho_local, x_table, precision=HIGHEST_PREC)
    section_data = swap_rows(section_data.reshape(y_rows, rows_px, zshare * 2 * xblock))
    section_data = section_data.reshape(points, zshare, 2, xblock)
    y_table = forward.reshape(2, points, 2, pieces, kyblock)
    section_data = jnp.einsum("yzrx,rysdk->zdksx", section_data, y_table, precision=HIGHEST_PREC)
    section_data = swap_depth(section_data.reshape(zshare, pieces, kyblock * 2 * xblock))
    section_data = section_data.reshape(pieces * zshare, kyblock, 2, xblock)
    source = jnp.arange(pieces * zshare, dtype=jnp.int32)
    device = source // zshare
    within = source % zshare
    z_order = device % rows_py * zblock + device // rows_py * zshare + within
    z_table = complex_table(z_order, every_index, points, -1.0)
    spectrum = jnp.einsum("zyrx,rzsk->kysx", section_data, z_table, precision=HIGHEST_PREC)
    q_depth, g_depth = freq_pair(every_index, points)
    ky_index = depth_index * kyblock + jnp.arange(kyblock, dtype=jnp.int32)
    q_col, g_col = freq_pair(ky_index, points)
    kx_index = px_index * xblock + jnp.arange(xblock, dtype=jnp.int32)
    q_row, g_row = freq_pair(kx_index, points)
    wave_unit = 2.0 * math.pi / (points * SPACING)
    squared = wave_unit**2 * (
        q_depth[:, None, None] ** 2 + q_col[None, :, None] ** 2 + q_row[None, None, :] ** 2
    )
    hartree = jnp.where(squared > 0, 4.0 * math.pi / jnp.where(squared > 0, squared, 1.0), 0.0)
    wave_z = wave_unit * g_depth[:, None, None]
    wave_y = wave_unit * g_col[None, :, None]
    wave_x = wave_unit * g_row[None, None, :]
    real_part = spectrum[:, :, 0, :]
    imag_part = spectrum[:, :, 1, :]
    first_factor = hartree - wave_x
    packed = jnp.stack(
        [
            jnp.stack([first_factor * real_part, first_factor * imag_part], 2),
            jnp.stack(
                [-wave_z * real_part - wave_y * imag_part, wave_y * real_part - wave_z * imag_part],
                2,
            ),
        ],
        0,
    )
    inverse = complex_table(every_index, every_index, points, 1.0)
    zi_table = complex_table(every_index, z_order, points, 1.0).reshape(
        2, points, 2, pieces, zshare
    )
    section_data = jnp.einsum("fkyrx,rksdz->ydfzsx", packed, zi_table, precision=HIGHEST_PREC)
    section_data = swap_depth(section_data.reshape(kyblock, pieces, 2 * zshare * 2 * xblock))
    section_data = section_data.reshape(points, 2, zshare, 2, xblock)
    yi_table = inverse.reshape(2, points, 2, rows_px, y_rows)
    section_data = jnp.einsum("kfzrx,rksby->xbfzsy", section_data, yi_table, precision=HIGHEST_PREC)
    section_data = swap_rows(section_data.reshape(xblock, rows_px, 2 * zshare * 2 * y_rows))
    section_data = section_data.reshape(points, 2, zshare, 2, y_rows)
    fields = jnp.einsum("kfzry,rksx->fszyx", section_data, inverse, precision=HIGHEST_PREC)
    fields = fields * (1.0 / float(points) ** 3)
    return fields.reshape(4, zshare, y_rows, points)


def body(orbitals, occupations, stick_map, core_density):
    bands_here, columns_here, doubled = orbitals.shape
    points = doubled // 2
    rows_px = lax.axis_size("px")
    rows_py = lax.axis_size("py")
    groups = lax.axis_size("band")
    px_index = lax.axis_index("px")
    py_index = lax.axis_index("py")
    xblock = points // rows_px
    zblock = points // rows_py
    y_rows = points // rows_px
    every_index = jnp.arange(points, dtype=jnp.int32)
    inverse = complex_table(every_index, every_index, points, 1.0)
    z_table = (
        inverse.reshape(2, points, 2, rows_py, zblock)
        .transpose(0, 1, 3, 2, 4)
        .reshape(doubled, doubled)
    )
    columns = jnp.dot(
        orbitals.astype(jnp.float32).reshape(bands_here * columns_here, doubled),
        z_table,
        precision=HIGHEST_PREC,
    )
    columns = columns.astype(jnp.bfloat16).reshape(bands_here, columns_here, doubled)
    columns = lax.all_to_all(columns, "py", split_axis=2, concat_axis=1, tiled=True)
    slot_index = stick_map[1] * xblock + (stick_map[0] - px_index * xblock)
    plane_data = (
        jnp.zeros((bands_here, points * xblock, 2 * zblock), jnp.float32)
        .at[:, slot_index]
        .set(columns.astype(jnp.float32))
    )
    plane_data = plane_data.reshape(bands_here, points, xblock, 2, zblock)
    plane_data = jnp.einsum("byxrz,rysk->bkxsz", plane_data, inverse, precision=HIGHEST_PREC)
    plane_data = plane_data.astype(jnp.bfloat16).reshape(bands_here, points, xblock * 2 * zblock)
    plane_data = lax.all_to_all(plane_data, "px", split_axis=1, concat_axis=2, tiled=True)
    plane_data = plane_data.astype(jnp.float32).reshape(bands_here, y_rows, points, 2, zblock)
    orbital_values = jnp.einsum("byxrz,rxsk->bszyk", plane_data, inverse, precision=HIGHEST_PREC)
    density = jnp.einsum(
        "b,bszyk->zyk", occupations, orbital_values * orbital_values, precision=HIGHEST_PREC
    )
    zshare = zblock // groups
    band_index = lax.axis_index("band")
    shared_rows = lax.psum_scatter(density, "band", scatter_dimension=0, tiled=True)
    core_rows = lax.dynamic_slice_in_dim(core_density, band_index * zshare, zshare, 0)
    rho_local = shared_rows + core_rows
    fields = transform(rho_local, groups * rows_py, band_index * rows_py + py_index, px_index)
    results = lax.all_gather(exchange_part(rho_local, fields), "band", axis=1, tiled=True)
    return (results[0], results[1:4])


def solution(mesh):
    return jax.shard_map(
        body,
        mesh=mesh,
        in_specs=(P("band", ("px", "py"), None), P("band"), P(None, "px"), P("py", "px", None)),
        out_specs=(P("py", "px", None), P(None, "py", "px", None)),
        check_vma=False,
    )
```

profile of v0, /device:TPU:0, one launch (start us, length us, event | category | flops | bytes accessed | tf_op | source)
XLA Modules:
  0.0 1160.9 jit_solution(13728535052132577211)
XLA Ops:
  27.8 12.3 %reshape.807 = f32[192,48,2,96]{3,2,1,0:T(2,128)} reshape(f32[9216,192]{1,0:T(8,128)} %scatter_custom_fusion) | data formatting | bytes 14155776 | tf_op jit(solution)/shard_map/reshape.2
  40.1 14.2 %copy.140 = f32[192,48,2,96]{0,3,2,1:T(8,128)} copy(f32[192,48,2,96]{3,2,1,0:T(2,128)} %reshape.807) | data formatting | bytes 14155776 | tf_op jit(solution)/shard_map/reshape.2
  54.3 18.6 %fusion.5 = bf16[1,192,48,2,96]{1,4,2,3,0:T(8,128)(2,1)} fusion(f32[192,48,2,96]{0,3,2,1:T(8,128)} %copy.140, f32[1,192,2,192]{3,1,0,2:T(8,128)S(1)} %get-tuple-element.11, f32[1,192,2,192]{3,1,0,2:T(8,128)S(1)} %get-tuple-element.10), kind=kOutput, calls=%fused_computation.8 | convolution fusion | flops 8155643904 | bytes 11206656 | tf_op jit(solution)/shard_map/byxrz,rysk->bkxsz/dot_general | solution.py:149
  72.8 11.6 copy.141
  84.4 24.4 %reshape.857 = bf16[1,192,9216]{2,0,1:T(2,128)(2,1)} reshape(bf16[1,192,48,2,96]{4,3,2,1,0:T(2,128)(2,1)} %copy.141) | data formatting | bytes 7077888 | tf_op jit(solution)/shard_map/reshape | solution.py:150
  108.8 78.5 %reduce.4 = bf16[192,9216]{1,0:T(8,128)(2,1)} reduce(bf16[192,1,9216]{2,1,0:T(2,128)(2,1)} %bitcast.221, bf16[]{:T(256)} %broadcast.1309), dimensions={1}, to_apply=%bitcast.207.reduce_sub_computation | reduce | bytes 7077890
  198.3 40.5 %all-to-all-done.1 = bf16[4,2,221184]{2,1,0:T(2,128)(2,1)} async-done(((bf16[4,2,221184]{2,1,0:T(2,128)(2,1)}), bf16[4,2,221184]{2,1,0:T(2,128)(2,1)}, u32[]{:S(2)}, u32[]{:S(2)}) %all-to-all-start.1) | async-done | bytes 3538976 | tf_op jit(solution)/shard_map/all_to_all | solution.py:151
  254.0 14.9 %reshape.809 = bf16[48,192,2,96]{3,2,1,0:T(2,128)(2,1)} reshape(bf16[1,48,4,9216]{3,2,1,0:T(4,128)(2,1)} %copy.143) | data formatting | bytes 7077888 | tf_op jit(solution)/shard_map/reshape.5
  268.9 10.5 fusion.2
  289.7 84.4 %reduce-scatter.2.cloned.1.call-done = f32[24,48,192]{2,1,0:T(8,128)} async-done(((f32[96,48,192]{2,1,0:T(8,128)}), f32[24,48,192]{2,1,0:T(8,128)}) %reduce-scatter.2.cloned.1.call-update) | async-done | bytes 884752 | tf_op jit(solution)/shard_map/reduce_scatter | solution.py:159
  380.9 7.5 copy.147
  388.4 9.3 reshape.811
  402.4 21.2 %all-to-all-done.2 = f32[48,4,2304]{2,0,1:T(8,128)S(1)} async-done(((f32[48,4,2304]{2,0,1:T(8,128)}), f32[48,4,2304]{2,0,1:T(8,128)S(1)}, u32[]{:S(2)}, u32[]{:S(2)}) %all-to-all-start.2) | async-done | bytes 1769504 | tf_op jit(solution)/shard_map/all_to_all | solution.py:30
  423.6 8.6 reshape.812
  432.2 10.4 fusion.27
  448.4 9.7 reshape.858
  466.9 37.3 %all-to-all-done.3 = f32[24,8,2304]{2,0,1:T(8,128)S(1)} async-done(((f32[24,8,2304]{2,0,1:T(8,128)}), f32[24,8,2304]{2,0,1:T(8,128)S(1)}, u32[]{:S(2)}, u32[]{:S(2)}) %all-to-all-start.3) | async-done | bytes 1769504 | tf_op jit(solution)/shard_map/all_to_all | solution.py:34
  504.1 8.6 reshape.814
  525.6 15.9 %fusion.22 = f32[24,8,2,24,2,48]{5,3,0,2,1,4:T(8,128)S(1)} fusion(f32[1,192,24,2,48]{1,4,2,3,0:T(8,128)S(1)} %maximum_bitcast_fusion.5, f32[1,192,24,2,48]{1,4,2,3,0:T(8,128)S(1)} %maximum_bitcast_fusion.4, f32[1,192,1,8,24]{1,4,0,3,2:T(8,128)S(1)} %copy-done.4, f32[1,192,1,8,24]{1,4,0,3,2:T(8,128)S(1)} %copy-done.3, ...), kind=kOutput, calls=%fused_computation.28 | convolution fusion | flops 4078190592 | bytes 7520256 | tf_op jit(solution)/shard_map/fkyrx,rksdz->ydfzsx/dot_general | solution.py:105
  541.5 8.0 copy.189
  549.5 16.6 %reshape.859 = f32[24,8,4608]{2,0,1:T(8,128)} reshape(f32[24,8,2,24,2,48]{5,4,3,2,0,1:T(2,128)} %copy.189) | data formatting | bytes 7077888 | tf_op jit(solution)/shard_map/reshape | solution.py:106
  571.5 77.6 %all-to-all-done.4 = f32[24,8,4608]{2,0,1:T(8,128)} async-done(((f32[24,8,4608]{2,0,1:T(8,128)}), f32[24,8,4608]{2,0,1:T(8,128)}, u32[]{:S(2)}, u32[]{:S(2)}) %all-to-all-start.4) | async-done | bytes 3538976 | tf_op jit(solution)/shard_map/all_to_all | solution.py:34
  649.2 17.3 %reshape.816 = f32[192,2,24,2,48]{4,3,2,1,0:T(2,128)} reshape(f32[8,24,1,4608]{3,1,0,2:T(8,128)} %bitcast.63) | data formatting | bytes 7077888 | tf_op jit(solution)/shard_map/reshape | solution.py:107
  666.5 24.9 %fusion.19 = f32[48,4,2,24,2,48]{0,5,3,2,1,4:T(8,128)} fusion(f32[192,2,24,2,48,1,1]{4,3,2,1,0,6,5:T(2,128)} %bitcast.218, f32[1,192,1,4,48]{1,4,0,3,2:T(8,128)S(1)} %get-tuple-element.20, f32[1,192,1,4,48]{1,4,0,3,2:T(8,128)S(1)} %get-tuple-element.19, f32[1,192,1,4,48]{1,4,0,3,2:T(8,128)S(1)} %get-tuple-element.18), kind=kOutput, calls=%fused_computation.27 | convolution fusion | flops 4077305856 | bytes 7520256 | tf_op jit(solution)/shard_map/kfzrx,rksby->xbfzsy/dot_general | solution.py:109
  691.4 13.7 %copy.157 = f32[48,4,2,24,2,48]{5,4,3,2,0,1:T(2,128)} copy(f32[48,4,2,24,2,48]{0,5,3,2,1,4:T(8,128)} %fusion.19) | data formatting | bytes 7077888 | tf_op jit(solution)/shard_map/kfzrx,rksby->xbfzsy/transpose | solution.py:109
  705.1 16.6 %reshape.817 = f32[48,4,4608]{2,0,1:T(8,128)} reshape(f32[48,4,2,24,2,48]{5,4,3,2,0,1:T(2,128)} %copy.157) | data formatting | bytes 7077888 | tf_op jit(solution)/shard_map/reshape | solution.py:110
  721.7 46.9 %all_to_all.84 = f32[48,4,4608]{2,0,1:T(8,128)} all-to-all(f32[48,4,4608]{2,0,1:T(8,128)} %reshape.817), channel_id=1, replica_groups=mesh['band'=4,'px'=4,'py'=2] {'px'}, dimensions={1} | all-to-all | bytes 7077888 | tf_op jit(solution)/shard_map/all_to_all | solution.py:30
  768.6 17.1 %reshape.818 = f32[192,2,24,2,48]{4,3,2,1,0:T(2,128)} reshape(f32[4,48,1,4608]{3,1,0,2:T(8,128)} %bitcast.224) | data formatting | bytes 7077888 | tf_op jit(solution)/shard_map/reshape | solution.py:111
  785.7 13.2 %copy.158 = f32[192,2,24,2,48]{0,4,3,2,1:T(8,128)} copy(f32[192,2,24,2,48]{4,3,2,1,0:T(2,128)} %reshape.818) | data formatting | bytes 7077888 | tf_op jit(solution)/shard_map/reshape | solution.py:111
  798.9 10.3 fusion.9
  816.6 320.4 %all-gather.2.cloned.1.call-done = f32[4,96,48,192]{3,2,1,0:T(8,128)} async-done(((f32[4,24,48,192]{3,2,1,0:T(8,128)}), f32[4,96,48,192]{3,2,1,0:T(8,128)}) %all-gather.2.cloned.1.call-update) | async-done | bytes 14155792 | tf_op jit(solution)/shard_map/all_gather | solution.py:163
  1141.8 11.8 %slice.55 = f32[3,96,48,192]{3,2,1,0:T(8,128)} slice(f32[4,96,48,192]{3,2,1,0:T(8,128)} %all-gather.2.cloned.1.call-done), slice={[1:4], [0:96], [0:48], [0:192]} | slice | bytes 21233664 | tf_op jit(solution)/shard_map/slice | solution.py:164
  (74 shorter events, 112.7 us)
Async XLA Ops:
  7.2 2.2 copy-start
  8.1 10.4 copy-start.5
  12.6 8.6 all-to-all-start
  192.9 45.9 %all-to-all-start.1 = ((bf16[4,2,221184]{2,1,0:T(2,128)(2,1)}), bf16[4,2,221184]{2,1,0:T(2,128)(2,1)}, u32[]{:S(2)}, u32[]{:S(2)}) async-start(bf16[4,2,221184]{2,1,0:T(2,128)(2,1)} %reshape.864), calls=%async_computation.1 | async-start | bytes 7077888 | tf_op jit(solution)/shard_map/all_to_all | solution.py:151
  197.6 176.5 %reduce-scatter.2.cloned.1.call-start = ((), (), s32[]{:S(2)}) async-start(), calls=%async_computation.7 | async-start | bytes 5898240 | tf_op jit(solution)/shard_map/reduce_scatter | solution.py:159
  397.7 25.9 %all-to-all-start.2 = ((f32[48,4,2304]{2,0,1:T(8,128)}), f32[48,4,2304]{2,0,1:T(8,128)S(1)}, u32[]{:S(2)}, u32[]{:S(2)}) async-start(f32[48,4,2304]{2,0,1:T(8,128)} %reshape.811), calls=%async_computation.3 | async-start | bytes 3538944 | tf_op jit(solution)/shard_map/all_to_all | solution.py:30
  458.1 46.0 %all-to-all-start.3 = ((f32[24,8,2304]{2,0,1:T(8,128)}), f32[24,8,2304]{2,0,1:T(8,128)S(1)}, u32[]{:S(2)}, u32[]{:S(2)}) async-start(f32[24,8,2304]{2,0,1:T(8,128)} %reshape.858), calls=%async_computation.4 | async-start | bytes 3538944 | tf_op jit(solution)/shard_map/all_to_all | solution.py:34
  524.6 0.9 copy-start.3
  524.6 1.0 copy-start.4
  566.1 83.1 %all-to-all-start.4 = ((f32[24,8,4608]{2,0,1:T(8,128)}), f32[24,8,4608]{2,0,1:T(8,128)}, u32[]{:S(2)}, u32[]{:S(2)}) async-start(f32[24,8,4608]{2,0,1:T(8,128)} %reshape.859), calls=%async_computation.5 | async-start | bytes 7077888 | tf_op jit(solution)/shard_map/all_to_all | solution.py:34
  570.6 566.4 %all-gather.2.cloned.1.call-start = ((), (), s32[]{:S(2)}) async-start(), calls=%async_computation.8 | async-start | bytes 23592960 | tf_op jit(solution)/shard_map/all_gather | solution.py:163
  809.6 1.3 copy-start.2
  1141.8 11.8 %copy-start.1 = (bf16[1,128,384]{2,1,0:T(8,128)(2,1)S(1)}, bf16[1,128,384]{2,1,0:T(8,128)(2,1)}, u32[]{:S(2)}) copy-start(bf16[1,128,384]{2,1,0:T(8,128)(2,1)} %param.4) | copy-start | bytes 294916
Sparse Core Ops, SparseCore 0:
  288.9 85.1 reduce-scatter.1
  816.7 320.2 all-gather.1
where the time goes:
time: 1170 us; the launch traced here: 1160 us
  waiting for transfers between devices  584 us (50%)
  local copies, waits for them, and re-layouts  291 us (25%)
  matrix products  103 us (9%)
  other arithmetic  98.1 us (8%)
  blocking collectives  46.9 us (4%)
  starting transfers between devices  22.4 us (2%)
  between operations  15.5 us (1%)
    all_gather x1, waiting for transfers between devices, body(): lax.all_gather(exchange_part(rho_local, fields), 'band', axis=1, tiled=True)  320 us
    all_to_all x2, waiting for transfers between devices, swap_depth(): lax.all_to_all(values, ('band', 'py'), split_axis=1, concat_axis=0, tiled...  115 us
    reduce_scatter x1, waiting for transfers between devices, body(): lax.psum_scatter(density, 'band', scatter_dimension=0, tiled=True)  84.4 us
    unnamed x2, other arithmetic  79.7 us
    all_to_all x1, blocking collectives, swap_rows(): return lax.all_to_all(values, 'px', split_axis=1, concat_axis=0, tiled=True)  46.9 us
    another operation x3, local copies, waits for them, and re-layouts  41.4 us
    all_to_all x1, waiting for transfers between devices, body(): lax.all_to_all(plane_data, 'px', split_axis=1, concat_axis=2, tiled=True)  40.5 us
    reshape x2, local copies, waits for them, and re-layouts, transform(): section_data = section_data.reshape(points, 2, zshare, 2, y_rows)  30.3 us
  transfers between devices with their start and end apart: 7, of which 7 were waited for; matrix products, arithmetic and copies ran while one was open for 1% of the time, Pallas kernels for 0%

commit v1 on v0

--- a/solution.py
+++ b/solution.py
@@ -3,6 +3,7 @@
 import jax.numpy as jnp
 from jax import lax
 from jax.sharding import PartitionSpec as P
+from jax.lax import all_to_all, psum
 
 SPACING = 0.25
 PBE_KAPPA = 0.804
@@ -31,7 +32,15 @@
 
 
 def swap_depth(values):
-    moved = lax.all_to_all(values, ("band", "py"), split_axis=1, concat_axis=0, tiled=True)
+    moved = jnp.concatenate(
+        all_to_all(
+            jnp.stack(jnp.split(values, psum(1, axis_name=("band", "py")), axis=1), 0),
+            axis_name=("band", "py"),
+            split_axis=0,
+            concat_axis=0,
+        ),
+        0,
+    )
     return moved
 
 

time: 1170 us -> 1220 us (1.043)
  local copies, waits for them, and re-layouts: 291 us -> 324 us
  other arithmetic: 98.1 us -> 116 us
    another operation x3 -> x8, local copies, waits for them, and re-layouts: 41.4 us -> 78.1 us
    reshape x3 -> x0, local copies, waits for them, and re-layouts: 31.6 us -> none  [the longest x1 17.3 us: transform(): section_data = section_data.reshape(points, 2, zshare, 2, xblock)]
    unnamed x18 -> x32, local copies, waits for them, and re-layouts: 19.5 us -> 47.4 us
    all_to_all x0 -> x2, other arithmetic: none -> 17.5 us  [swap_depth(): all_to_all(jnp.stack(jnp.split(values, psum(1, axis_name=('band', 'py')),...]
    transpose x0 -> x2, local copies, waits for them, and re-layouts: none -> 14.8 us  [the longest x1 8.97 us: transform(): jnp.einsum('fkyrx,rksdz->ydfzsx', packed, zi_table, precision=HIGHEST_PREC)]
    reshape x2 -> x1, local copies, waits for them, and re-layouts: 24.6 us -> 16.6 us  [transform(): section_data.reshape(kyblock, pieces, 2 * zshare * 2 * xblock)]
where the time goes in v1:
time: 1220 us; the launch traced here: 1210 us
  waiting for transfers between devices  584 us (48%)
  local copies, waits for them, and re-layouts  324 us (27%)
  other arithmetic  116 us (10%)
  matrix products  103 us (8%)
  blocking collectives  46.8 us (4%)
  starting transfers between devices  22.6 us (2%)
  between operations  15.3 us (1%)
    all_gather x1, waiting for transfers between devices, body(): lax.all_gather(exchange_part(rho_local, fields), 'band', axis=1, tiled=True)  320 us
    all_to_all x2, waiting for transfers between devices, swap_depth(): all_to_all(jnp.stack(jnp.split(values, psum(1, axis_name=('band', 'py')),...  115 us
    reduce_scatter x1, waiting for transfers between devices, body(): lax.psum_scatter(density, 'band', scatter_dimension=0, tiled=True)  84.4 us
    unnamed x2, other arithmetic  79.6 us
    unnamed x32, local copies, waits for them, and re-layouts  47.4 us
    all_to_all x1, blocking collectives, swap_rows(): return lax.all_to_all(values, 'px', split_axis=1, concat_axis=0, tiled=True)  46.8 us
    another operation x3, local copies, waits for them, and re-layouts  41.4 us
    all_to_all x1, waiting for transfers between devices, body(): lax.all_to_all(plane_data, 'px', split_axis=1, concat_axis=2, tiled=True)  40.5 us
  transfers between devices with their start and end apart: 7, of which 7 were waited for; matrix products, arithmetic and copies ran while one was open for 1% of the time, Pallas kernels for 0%

profile of v1, /device:TPU:0, one launch (start us, length us, event | category | flops | bytes accessed | tf_op | source)
XLA Modules:
  0.0 1211.5 jit_solution(542931258034393094)
XLA Ops:
  28.2 12.3 %reshape.799 = f32[192,48,2,96]{3,2,1,0:T(2,128)} reshape(f32[9216,192]{1,0:T(8,128)} %scatter_custom_fusion) | data formatting | bytes 14155776 | tf_op jit(solution)/shard_map/reshape.2
  40.4 14.2 %copy.144 = f32[192,48,2,96]{0,3,2,1:T(8,128)} copy(f32[192,48,2,96]{3,2,1,0:T(2,128)} %reshape.799) | data formatting | bytes 14155776 | tf_op jit(solution)/shard_map/reshape.2
  54.6 18.6 %fusion.5 = bf16[1,192,48,2,96]{1,4,2,3,0:T(8,128)(2,1)} fusion(f32[192,48,2,96]{0,3,2,1:T(8,128)} %copy.144, f32[1,192,2,192]{3,1,0,2:T(8,128)S(1)} %get-tuple-element.11, f32[1,192,2,192]{3,1,0,2:T(8,128)S(1)} %get-tuple-element.10), kind=kOutput, calls=%fused_computation.8 | convolution fusion | flops 8155643904 | bytes 11206656 | tf_op jit(solution)/shard_map/byxrz,rysk->bkxsz/dot_general | solution.py:158
  73.2 11.6 copy.145
  84.8 24.4 %reshape.847 = bf16[1,192,9216]{2,0,1:T(2,128)(2,1)} reshape(bf16[1,192,48,2,96]{4,3,2,1,0:T(2,128)(2,1)} %copy.145) | data formatting | bytes 7077888 | tf_op jit(solution)/shard_map/reshape | solution.py:159
  109.2 78.3 %reduce.6 = bf16[192,9216]{1,0:T(8,128)(2,1)} reduce(bf16[192,1,9216]{2,1,0:T(2,128)(2,1)} %bitcast.267, bf16[]{:T(256)} %broadcast.1311), dimensions={1}, to_apply=%bitcast.253.reduce_sub_computation | reduce | bytes 7077890
  198.5 40.5 %all-to-all-done.1 = bf16[4,2,221184]{2,1,0:T(2,128)(2,1)} async-done(((bf16[4,2,221184]{2,1,0:T(2,128)(2,1)}), bf16[4,2,221184]{2,1,0:T(2,128)(2,1)}, u32[]{:S(2)}, u32[]{:S(2)}) %all-to-all-start.1) | async-done | bytes 3538976 | tf_op jit(solution)/shard_map/all_to_all | solution.py:160
  254.2 14.9 %reshape.801 = bf16[48,192,2,96]{3,2,1,0:T(2,128)(2,1)} reshape(bf16[1,48,4,9216]{3,2,1,0:T(4,128)(2,1)} %copy.147) | data formatting | bytes 7077888 | tf_op jit(solution)/shard_map/reshape.5
  269.2 10.6 fusion.2
  290.0 84.4 %reduce-scatter.2.cloned.1.call-done = f32[24,48,192]{2,1,0:T(8,128)} async-done(((f32[96,48,192]{2,1,0:T(8,128)}), f32[24,48,192]{2,1,0:T(8,128)}) %reduce-scatter.2.cloned.1.call-update) | async-done | bytes 884752 | tf_op jit(solution)/shard_map/reduce_scatter | solution.py:168
  388.6 9.3 reshape.803
  402.9 21.2 %all-to-all-done.2 = f32[48,4,2304]{2,0,1:T(8,128)S(1)} async-done(((f32[48,4,2304]{2,0,1:T(8,128)}), f32[48,4,2304]{2,0,1:T(8,128)S(1)}, u32[]{:S(2)}, u32[]{:S(2)}) %all-to-all-start.2) | async-done | bytes 1769504 | tf_op jit(solution)/shard_map/all_to_all | solution.py:31
  424.1 8.6 reshape.804
  432.6 10.4 fusion.27
  448.9 8.6 reshape.805
  473.2 37.2 %all-to-all-done.3 = f32[8,24,1,2304]{3,2,1,0:T(1,128)S(1)} async-done(((f32[8,24,1,2304]{3,2,1,0:T(1,128)}), f32[8,24,1,2304]{3,2,1,0:T(1,128)S(1)}, u32[]{:S(2)}, u32[]{:S(2)}) %all-to-all-start.3) | async-done | bytes 1769504 | tf_op jit(solution)/shard_map/all_to_all | solution.py:36
  516.3 9.6 reshape_reshape.6
  539.1 15.7 %fusion.22 = f32[24,8,2,24,2,48]{5,3,0,2,1,4:T(8,128)S(1)} fusion(f32[1,192,24,2,48]{1,4,2,3,0:T(8,128)S(1)} %maximum_bitcast_fusion.5, f32[1,192,24,2,48]{1,4,2,3,0:T(8,128)S(1)} %maximum_bitcast_fusion.4, f32[1,192,1,8,24]{1,4,0,3,2:T(8,128)S(1)} %copy-done.4, f32[1,192,1,8,24]{1,4,0,3,2:T(8,128)S(1)} %copy-done.3, ...), kind=kOutput, calls=%fused_computation.28 | convolution fusion | flops 4078190592 | bytes 7520256 | tf_op jit(solution)/shard_map/fkyrx,rksdz->ydfzsx/dot_general | solution.py:114
  554.8 9.0 copy.157
  563.7 16.6 %reshape.806 = f32[24,8,4608]{2,1,0:T(8,128)} reshape(f32[24,8,2,24,2,48]{5,4,3,2,1,0:T(2,128)} %copy.157) | data formatting | bytes 7077888 | tf_op jit(solution)/shard_map/reshape | solution.py:115
  610.8 77.6 %all-to-all-done.4 = f32[8,24,1,4608]{3,2,1,0:T(1,128)} async-done(((f32[8,24,1,4608]{3,2,1,0:T(1,128)}), f32[8,24,1,4608]{3,2,1,0:T(1,128)}, u32[]{:S(2)}, u32[]{:S(2)}) %all-to-all-start.4) | async-done | bytes 3538976 | tf_op jit(solution)/shard_map/all_to_all | solution.py:36
  688.4 11.6 reduce.4
  700.1 17.1 %reshape_reshape.7 = f32[192,2,24,2,48]{4,3,2,1,0:T(2,128)} reshape(f32[8,24,4608]{2,1,0:T(8,128)} %reduce.4) | data formatting | bytes 7077888 | tf_op jit(solution)/shard_map/reshape;reshape | solution.py:116
  717.2 25.0 %fusion.19 = f32[48,4,2,24,2,48]{0,5,3,2,1,4:T(8,128)} fusion(f32[192,2,24,2,48,1,1]{4,3,2,1,0,6,5:T(2,128)} %bitcast.264, f32[1,192,1,4,48]{1,4,0,3,2:T(8,128)S(1)} %get-tuple-element.20, f32[1,192,1,4,48]{1,4,0,3,2:T(8,128)S(1)} %get-tuple-element.19, f32[1,192,1,4,48]{1,4,0,3,2:T(8,128)S(1)} %get-tuple-element.18), kind=kOutput, calls=%fused_computation.27 | convolution fusion | flops 4077305856 | bytes 7520256 | tf_op jit(solution)/shard_map/kfzrx,rksby->xbfzsy/dot_general | solution.py:118
  742.1 13.7 %copy.159 = f32[48,4,2,24,2,48]{5,4,3,2,0,1:T(2,128)} copy(f32[48,4,2,24,2,48]{0,5,3,2,1,4:T(8,128)} %fusion.19) | data formatting | bytes 7077888 | tf_op jit(solution)/shard_map/kfzrx,rksby->xbfzsy/transpose | solution.py:118
  755.9 16.6 %reshape.807 = f32[48,4,4608]{2,0,1:T(8,128)} reshape(f32[48,4,2,24,2,48]{5,4,3,2,0,1:T(2,128)} %copy.159) | data formatting | bytes 7077888 | tf_op jit(solution)/shard_map/reshape | solution.py:119
  772.5 46.8 %all_to_all.64 = f32[48,4,4608]{2,0,1:T(8,128)} all-to-all(f32[48,4,4608]{2,0,1:T(8,128)} %reshape.807), channel_id=1, replica_groups=mesh['band'=4,'px'=4,'py'=2] {'px'}, dimensions={1} | all-to-all | bytes 7077888 | tf_op jit(solution)/shard_map/all_to_all | solution.py:31
  819.3 17.1 %reshape.808 = f32[192,2,24,2,48]{4,3,2,1,0:T(2,128)} reshape(f32[4,48,1,4608]{3,1,0,2:T(8,128)} %bitcast.270) | data formatting | bytes 7077888 | tf_op jit(solution)/shard_map/reshape | solution.py:120
  836.4 13.2 %copy.160 = f32[192,2,24,2,48]{0,4,3,2,1:T(8,128)} copy(f32[192,2,24,2,48]{4,3,2,1,0:T(2,128)} %reshape.808) | data formatting | bytes 7077888 | tf_op jit(solution)/shard_map/reshape | solution.py:120
  849.6 10.3 fusion.9
  867.3 320.4 %all-gather.2.cloned.1.call-done = f32[4,96,48,192]{3,2,1,0:T(8,128)} async-done(((f32[4,24,48,192]{3,2,1,0:T(8,128)}), f32[4,96,48,192]{3,2,1,0:T(8,128)}) %all-gather.2.cloned.1.call-update) | async-done | bytes 14155792 | tf_op jit(solution)/shard_map/all_gather | solution.py:172
  1192.6 11.8 slice.55
  (92 shorter events, 158.8 us)
Async XLA Ops:
  7.2 2.2 copy-start
  8.1 10.5 copy-start.5
  12.8 8.6 all-to-all-start
  193.1 45.9 %all-to-all-start.1 = ((bf16[4,2,221184]{2,1,0:T(2,128)(2,1)}), bf16[4,2,221184]{2,1,0:T(2,128)(2,1)}, u32[]{:S(2)}, u32[]{:S(2)}) async-start(bf16[4,2,221184]{2,1,0:T(2,128)(2,1)} %reshape.854), calls=%async_computation.1 | async-start | bytes 7077888 | tf_op jit(solution)/shard_map/all_to_all | solution.py:160
  197.8 176.6 %reduce-scatter.2.cloned.1.call-start = ((), (), s32[]{:S(2)}) async-start(), calls=%async_computation.7 | async-start | bytes 5898240 | tf_op jit(solution)/shard_map/reduce_scatter | solution.py:168
  398.0 26.1 %all-to-all-start.2 = ((f32[48,4,2304]{2,0,1:T(8,128)}), f32[48,4,2304]{2,0,1:T(8,128)S(1)}, u32[]{:S(2)}, u32[]{:S(2)}) async-start(f32[48,4,2304]{2,0,1:T(8,128)} %reshape.803), calls=%async_computation.3 | async-start | bytes 3538944 | tf_op jit(solution)/shard_map/all_to_all | solution.py:31
  464.4 46.0 %all-to-all-start.3 = ((f32[8,24,1,2304]{3,2,1,0:T(1,128)}), f32[8,24,1,2304]{3,2,1,0:T(1,128)S(1)}, u32[]{:S(2)}, u32[]{:S(2)}) async-start(f32[8,24,1,2304]{3,2,1,0:T(1,128)} %fusion.82), calls=%async_computation.4 | async-start | bytes 3538944 | tf_op jit(solution)/shard_map/all_to_all | solution.py:36
  538.0 0.9 copy-start.3
  538.1 1.0 copy-start.4
  605.4 83.1 %all-to-all-start.4 = ((f32[8,24,1,4608]{3,2,1,0:T(1,128)}), f32[8,24,1,4608]{3,2,1,0:T(1,128)}, u32[]{:S(2)}, u32[]{:S(2)}) async-start(f32[8,24,1,4608]{3,2,1,0:T(1,128)} %fusion.72), calls=%async_computation.5 | async-start | bytes 7077888 | tf_op jit(solution)/shard_map/all_to_all | solution.py:36
  609.9 577.9 %all-gather.2.cloned.1.call-start = ((), (), s32[]{:S(2)}) async-start(), calls=%async_computation.8 | async-start | bytes 23592960 | tf_op jit(solution)/shard_map/all_gather | solution.py:172
  860.3 1.3 copy-start.2
  1192.6 11.8 copy-start.1
Sparse Core Ops, SparseCore 0:
  289.2 85.1 reduce-scatter.1
  867.5 320.2 all-gather.1
